TPU v7x, 32 devices: a whole 2x2x4 slice. The times are simulated.
32 devices in a mesh: seq: 8 (over z, y), batch: 4 (over x, core).
Axes of the slice: x: 2, y: 2, z: 4, core: 2. Of those that a mesh axis runs over, the one named last changes fastest.
Arguments:
- q_nope: bfloat16 [4, 64, 128, 128], P('batch', None, 'seq'), may hold values from -6 to 6
- q_rope: bfloat16 [4, 64, 128, 64], P('batch', None, 'seq'), may hold values from -8 to 8
- absorb_k: bfloat16 [128, 128, 512], P('seq'), may hold values from -0.5 to 0.5
- absorb_v: bfloat16 [128, 512, 128], P('seq'), may hold values from -0.25 to 0.25
- cache_latent: bfloat16 [4, 8192, 512], P('batch', 'seq'), may hold values from -6 to 6
- cache_rope: bfloat16 [4, 8192, 64], P('batch', 'seq'), may hold values from -8 to 8
- draft_latent: bfloat16 [4, 64, 512], P('batch'), may hold values from -6 to 6
- draft_rope: bfloat16 [4, 64, 64], P('batch'), may hold values from -6 to 6
- residual: bfloat16 [256, 7168], P('batch', 'seq'), may hold values from -1.2 to 1.2
- out_proj: bfloat16 [16384, 7168], P('seq'), may hold values from -0.046875 to 0.046875
- norm_gain: float32 [7168], replicated, may hold values from 0.5 to 1.5
- lm_head: bfloat16 [65536, 7168], P(('seq', 'batch')), may hold values from -2.4095235 to 2.4095235
- parent: int32 [4, 64], replicated, may hold values from 0 to 62, as said below
- draft_ids: int32 [4, 64], replicated, may hold values from 0 to 65535
- cache_len: int32 [4], P('batch'), may hold values from 2048 to 8192
- accept_len: int32 [4], P('batch'), may hold values from 1 to 64
Outputs:
- hidden_out: bfloat16 [256, 7168], P('batch', 'seq')
- target_logp: float32 [4, 64], P('batch')
- accepted_score: float32 [4], P('batch')
Inputs may be any that keep to these rules, and one draw needn't show every extreme that they name: parent[b, 0] = 0, and 0 <= parent[b, i] < i for i >= 1.
All inputs are finite; a program needn't handle non-finite values.
Results may differ from a plain program's by a relative error of at most 0.0095.
Values may be sent and summed in bfloat16 or wider, within the bound.
No kernel may reach another device: no remote copies, remote signals or barrier semaphores. Data moves between devices by JAX's collectives and lax.ppermute only.
A program may use at most 256 MiB of HBM per device.

v0:
```python
import math
import jax
import jax.numpy as jnp
from jax import lax
from jax.sharding import PartitionSpec as P

masked_value = -1e30
norm_epsilon = 1e-06
highest = lax.Precision.HIGHEST


def ancestry_of(parents):
    draft_count = parents.shape[1]
    indices = jnp.arange(draft_count, dtype=jnp.int32)
    parent_map = (
        (parents[:, :, None] == indices[None, None, :]) & (indices[None, :, None] > 0)
    ).astype(jnp.float32)
    ancestry = jnp.broadcast_to(jnp.eye(draft_count, dtype=jnp.float32), parent_map.shape)
    for doubling in range(draft_count.bit_length() - 1):
        ancestry = ancestry + jnp.einsum("rij,rjk->rik", ancestry, parent_map, precision=highest)
        parent_map = jnp.einsum("rij,rjk->rik", parent_map, parent_map, precision=highest)
    return ancestry > 0.5


def body(
    q_nope,
    q_rope,
    absorb_k,
    absorb_v,
    cache_latent,
    cache_rope,
    draft_latent,
    draft_rope,
    residual,
    out_proj,
    norm_gain,
    lm_head,
    parent,
    draft_ids,
    cache_len,
    accept_len,
):
    requests, draft_count, local_heads, nope_width = q_nope.shape
    cache_rows = cache_latent.shape[1]
    score_scale = 1.0 / math.sqrt(nope_width + q_rope.shape[3])
    seq_index = lax.axis_index("seq")
    batch_index = lax.axis_index("batch")
    query_latent = jnp.einsum(
        "rihn,hnc->rihc", q_nope, absorb_k, preferred_element_type=jnp.float32
    ).astype(jnp.bfloat16)
    query_all, rope_all = (
        lax.all_gather(query_latent, "seq", axis=2, tiled=True),
        lax.all_gather(q_rope, "seq", axis=2, tiled=True),
    )
    cache_scores = jnp.einsum(
        "rihc,rtc->rhit", query_all, cache_latent, preferred_element_type=jnp.float32
    )
    cache_scores = cache_scores + jnp.einsum(
        "rihe,rte->rhit", rope_all, cache_rope, preferred_element_type=jnp.float32
    )
    positions = seq_index * cache_rows + jnp.arange(cache_rows, dtype=jnp.int32)
    in_cache = positions[None, :] < cache_len[:, None]
    cache_scores = jnp.where(in_cache[:, None, None, :], cache_scores * score_scale, masked_value)
    tree_scores = jnp.einsum(
        "rihc,rjc->rhij", query_all, draft_latent, preferred_element_type=jnp.float32
    )
    tree_scores = tree_scores + jnp.einsum(
        "rihe,rje->rhij", rope_all, draft_rope, preferred_element_type=jnp.float32
    )
    own_parents = lax.dynamic_slice_in_dim(parent, batch_index * requests, requests, 0)
    ancestry = ancestry_of(own_parents)
    tree_scores = jnp.where(ancestry[:, None, :, :], tree_scores * score_scale, masked_value)
    local_top = jnp.maximum(jnp.max(cache_scores, axis=3), jnp.max(tree_scores, axis=3))
    row_top = lax.pmax(local_top, "seq")
    cache_weights = jnp.exp(cache_scores - row_top[..., None])
    weight_sum = jnp.sum(cache_weights, axis=3)
    partial_value = jnp.einsum(
        "rhit,rtc->rhic",
        cache_weights.astype(jnp.bfloat16),
        cache_latent,
        preferred_element_type=jnp.float32,
    )
    head_first = seq_index * local_heads
    tree_mine = lax.dynamic_slice_in_dim(tree_scores, head_first, local_heads, 1)
    top_mine = lax.dynamic_slice_in_dim(row_top, head_first, local_heads, 1)
    tree_weights = jnp.exp(tree_mine - top_mine[..., None])
    tree_out = jnp.einsum(
        "rhij,rjc->rhic",
        tree_weights.astype(jnp.bfloat16),
        draft_latent,
        preferred_element_type=jnp.float32,
    )
    projected = jnp.einsum(
        "rhic,hcn->rhin",
        partial_value,
        lax.all_gather(absorb_v, "seq", axis=0, tiled=True),
        preferred_element_type=jnp.float32,
    )
    summed, weight_total = (
        lax.psum_scatter(projected, "seq", scatter_dimension=1, tiled=True),
        lax.psum_scatter(weight_sum, "seq", scatter_dimension=1, tiled=True),
    )
    summed = summed + jnp.einsum(
        "rhic,hcn->rhin", tree_out, absorb_v, preferred_element_type=jnp.float32
    )
    weight_total = weight_total + jnp.sum(tree_weights, axis=3)
    head_out = (summed / weight_total[..., None]).astype(jnp.bfloat16)
    head_rows = jnp.transpose(head_out, (0, 2, 1, 3)).reshape(
        requests * draft_count, local_heads * head_out.shape[3]
    )
    branch_term = jnp.dot(head_rows, out_proj, preferred_element_type=jnp.float32)
    width_local = residual.shape[1]
    feature_first = seq_index * width_local
    stream_mine = residual.astype(jnp.float32) + lax.psum_scatter(
        branch_term, "seq", scatter_dimension=1, tiled=True
    )
    square = lax.psum(jnp.sum(stream_mine * stream_mine, axis=1), "seq")
    width_all = width_local * lax.axis_size("seq")
    gain_mine = lax.dynamic_slice_in_dim(norm_gain, feature_first, width_local, 0)
    normed_mine = (
        stream_mine * lax.rsqrt(square / width_all + norm_epsilon)[:, None] * gain_mine
    ).astype(jnp.bfloat16)
    normed = lax.all_gather(normed_mine, "seq", axis=1, tiled=True)
    hidden_out = stream_mine.astype(jnp.bfloat16)
    vocab_rows = lm_head.shape[0]
    vocab_first = lax.axis_index(("seq", "batch")) * vocab_rows
    logits = jnp.einsum(
        "rd,vd->rv",
        lax.all_gather(normed, "batch", axis=0, tiled=True),
        lm_head,
        preferred_element_type=jnp.float32,
    )
    request_total = parent.shape[0]
    parent_rows = (
        jnp.arange(request_total, dtype=jnp.int32)[:, None] * draft_count + parent
    ).reshape(-1)
    source = logits[parent_rows]
    column = jnp.arange(vocab_rows, dtype=jnp.int32) + vocab_first
    picked = jnp.sum(
        jnp.where(column[None, :] == draft_ids.reshape(-1)[:, None], source, 0.0), axis=1
    )
    local_best = jnp.max(logits, axis=1)
    best = lax.pmax(local_best, ("seq", "batch"))
    exp_mass, chosen = lax.psum(
        (jnp.sum(jnp.exp(logits - best[:, None]), axis=1), picked), ("seq", "batch")
    )
    log_total = best + jnp.log(exp_mass)
    target_all = (chosen - log_total[parent_rows]).reshape(request_total, draft_count)
    target_logp = lax.dynamic_slice_in_dim(target_all, batch_index * requests, requests, 0)
    accepted_score = jnp.sum(
        jnp.where(
            jnp.arange(draft_count, dtype=jnp.int32)[None, :] < accept_len[:, None],
            target_logp,
            0.0,
        ),
        axis=1,
    )
    return (hidden_out, target_logp, accepted_score)


def solution(mesh):
    in_specs = (
        P("batch", None, "seq", None),
        P("batch", None, "seq", None),
        P("seq", None, None),
        P("seq", None, None),
        P("batch", "seq", None),
        P("batch", "seq", None),
        P("batch", None, None),
        P("batch", None, None),
        P("batch", "seq"),
        P("seq", None),
        P(),
        P(("seq", "batch"), None),
        P(),
        P(),
        P("batch"),
        P("batch"),
    )
    out_specs = (P("batch", "seq"), P("batch", None), P("batch"))
    return jax.shard_map(body, mesh=mesh, in_specs=in_specs, out_specs=out_specs, check_vma=False)
```

profile of v0, /device:TPU:0, one launch (start us, length us, event | category | flops | bytes accessed | tf_op | source)
XLA Modules:
  0.0 851.1 jit_solution(5020924196684965757)
XLA Ops:
  7.2 1.9 copy.79
  9.1 0.0 all-gather.5.cloned.1.call-start
  9.2 2.4 fusion.25
  11.6 0.0 all-gather.9.cloned.1.call-start
  11.7 0.7 all-gather.9.cloned.1.call-update
  12.3 0.0 reduce-scatter.6.cloned.1.call-start
  12.4 0.2 fusion.68
  12.6 0.2 convolution_add_fusion.5
  12.9 0.2 fusion.81
  13.0 0.2 convolution_add_fusion.4
  13.2 0.2 fusion.82
  13.4 0.2 convolution_add_fusion.3
  13.5 0.2 fusion.83
  13.7 0.2 convolution_add_fusion.2
  13.9 0.2 fusion.84
  14.0 0.2 convolution_add_fusion.1
  14.2 0.2 fusion.41
  14.4 0.1 copy.82
  15.2 46.8 %all-gather.7.cloned.1.call-done = bf16[1,64,128,64]{3,1,0,2:T(8,128)(2,1)} async-done(((bf16[1,64,16,64]{3,1,0,2:T(8,128)(2,1)}), bf16[1,64,128,64]{3,1,0,2:T(8,128)(2,1)}) %all-gather.7.cloned.1.call-update) | async-done | bytes 1048592 | tf_op jit(solution)/shard_map/all_gather | solution.py:53
  62.0 3.5 copy.80
  65.5 4.1 fusion.20
  69.6 13.3 %fusion.42 = f32[1024,64,128]{0,2,1:T(8,128)} fusion(bf16[1,64,128,64]{2,3,1,0:T(8,128)(2,1)S(1)} %copy.80, bf16[1,1024,64]{1,2,0:T(8,128)(2,1)S(1)} %copy-done.7), kind=kOutput, calls=%fused_computation.42 | convolution fusion | flops 1073741824 | bytes 34734080 | tf_op jit(solution)/shard_map/rihe,rte->rhit/dot_general | solution.py:58
  82.9 104.3 %all-gather.5.cloned.1.call-done = bf16[1,64,128,512]{3,1,0,2:T(8,128)(2,1)} async-done(((bf16[1,64,16,512]{3,1,0,2:T(8,128)(2,1)}), bf16[1,64,128,512]{3,1,0,2:T(8,128)(2,1)}) %all-gather.5.cloned.1.call-update) | async-done | bytes 8388624 | tf_op jit(solution)/shard_map/all_gather | solution.py:52
  187.1 10.7 %fusion.79 = (f32[128,64]{1,0:T(8,128)S(1)}, f32[1,128,64,64]{2,3,1,0:T(8,128)}) fusion(f32[64,64,128]{1,0,2:T(8,128)} %fusion.20, bf16[1,64,512]{2,1,0:T(8,128)(2,1)S(1)} %copy-done.8, bf16[1,64,128,512]{3,1,0,2:T(8,128)(2,1)} %all-gather.5.cloned.1.call-done, pred[64,64]{0,1:T(8,128)(4,1)S(1)} %copy.82), kind=kOutput, calls=%fused_computation.93 | convolution fusion | flops 538959872 | bytes 12685312 | tf_op jit(solution)/shard_map/rihc,rjc->rhij/dot_general | solution.py:64
  197.8 0.1 copy.85
  197.9 32.5 %bitcast_reduce_fusion = (f32[128,64]{0,1:T(8,128)S(1)}, f32[1,1024,64,128]{1,3,2,0:T(8,128)}) fusion(f32[1024,64,128]{0,2,1:T(8,128)} %fusion.42, bf16[1,1024,512]{2,1,0:T(8,128)(2,1)S(1)} %copy-done.5, bf16[1,64,128,512]{3,1,0,2:T(8,128)(2,1)} %all-gather.5.cloned.1.call-done, pred[1024]{0:T(1024)(128)(4,1)S(1)} %add_compare_fusion), kind=kOutput, calls=%fused_computation.3 | convolution fusion | flops 8623480832 | bytes 76579840 | tf_op jit(solution)/shard_map/rihc,rtc->rhit/dot_general | solution.py:55
  230.4 37.2 %pmax.14 = f32[1,128,64]{1,2,0:T(8,128)S(1)} all-reduce(f32[1,128,64]{1,2,0:T(8,128)S(1)} %maximum_bitcast_fusion), channel_id=1, replica_groups=mesh['seq'=8,'batch'=4] {'seq'}, use_global_device_ids=true, to_apply=%region_2.3 | all-reduce | flops 8192 | bytes 65536 | tf_op jit(solution)/shard_map/pmax | solution.py:74
  267.6 19.6 %fusion.2 = (f32[128,64]{0,1:T(8,128)S(1)}, bf16[128,64,1024]{2,0,1:T(8,128)(2,1)}) fusion(f32[1,1024,64,128]{1,3,2,0:T(8,128)} %get-tuple-element.12, f32[128,64]{0,1:T(8,128)S(1)} %bitcast.160), kind=kLoop, calls=%fused_computation.8 | loop fusion | flops 25157632 | bytes 50397184 | tf_op jit(solution)/shard_map/reduce_sum | solution.py:76
  287.2 0.7 copy.89
  287.9 0.0 reduce-scatter.4.cloned.1.call-start
  288.0 127.4 %all-gather.9.cloned.1.call-done = bf16[128,512,128]{2,1,0:T(8,128)(2,1)} async-done(((bf16[16,512,128]{2,1,0:T(8,128)(2,1)}), bf16[128,512,128]{2,1,0:T(8,128)(2,1)}) %all-gather.9.cloned.1.call-update) | async-done | bytes 16777232 | tf_op jit(solution)/shard_map/all_gather | solution.py:96
  415.4 27.1 %fusion.17 = f32[1,128,64,128]{3,2,1,0:T(8,128)} fusion(bf16[128,512,128]{2,1,0:T(8,128)(2,1)} %all-gather.9.cloned.1.call-done, bf16[128,64,1024]{2,0,1:T(8,128)(2,1)} %get-tuple-element.8, bf16[1,1024,512]{2,1,0:T(8,128)(2,1)S(1)} %copy-done.5), kind=kOutput, calls=%fused_computation.21 | convolution fusion | flops 9663676416 | bytes 38797312 | tf_op jit(solution)/shard_map/rhic,hcn->rhin/dot_general | solution.py:93
  442.5 0.0 reduce-scatter.8.cloned.1.call-start
  442.6 0.1 constant_dynamic-slice_fusion.1
  442.6 0.1 copy.87
  442.7 1.3 fusion.47
  444.0 0.1 copy.100
  444.1 35.8 %reduce-scatter.6.cloned.1.call-done = f32[1,16,64]{2,0,1:T(1,128)} async-done(((f32[1,128,64]{2,0,1:T(1,128)}), f32[1,16,64]{2,0,1:T(1,128)}) %reduce-scatter.6.cloned.1.call-update) | async-done | bytes 4112 | tf_op jit(solution)/shard_map/reduce_scatter | solution.py:101
  479.9 0.8 copy.91
  480.6 0.1 copy.92
  480.7 90.0 %reduce-scatter.4.cloned.1.call-done = f32[1,16,64,128]{3,2,1,0:T(8,128)} async-done(((f32[1,128,64,128]{3,2,1,0:T(8,128)}), f32[1,16,64,128]{3,2,1,0:T(8,128)}) %reduce-scatter.4.cloned.1.call-update) | async-done | bytes 524304 | tf_op jit(solution)/shard_map/reduce_scatter | solution.py:100
  570.7 2.0 fusion.38
  572.7 0.2 copy.93
  572.9 13.5 %fusion.52 = f32[64,7168]{1,0:T(8,128)} fusion(bf16[2048,7168]{1,0:T(8,128)(2,1)} %param.25, bf16[8,8,16,128]{3,2,1,0:T(8,128)(2,1)S(1)} %bitcast.159), kind=kOutput, calls=%fused_computation.50 | convolution fusion | flops 1879048192 | bytes 31457280 | tf_op jit(solution)/shard_map/dot_general | solution.py:111
  586.4 0.0 all-gather.11.cloned.1.call-start
  586.5 0.8 dynamic_slice.18
  587.3 65.9 %reduce-scatter.8.cloned.1.call-done = f32[64,896]{1,0:T(8,128)} async-done(((f32[64,7168]{1,0:T(8,128)}), f32[64,896]{1,0:T(8,128)}) %reduce-scatter.8.cloned.1.call-update) | async-done | bytes 229392 | tf_op jit(solution)/shard_map/reduce_scatter | solution.py:114
  653.2 1.1 multiply_reduce_fusion
  654.2 19.4 %psum.21 = f32[64]{0:T(128)S(1)} all-reduce(f32[64]{0:T(128)S(1)} %multiply_reduce_fusion), channel_id=1, replica_groups=mesh['seq'=8,'batch'=4] {'seq'}, use_global_device_ids=true, to_apply=%region_9.10 | all-reduce | flops 64 | bytes 512 | tf_op jit(solution)/shard_map/psum | solution.py:117
  673.6 1.6 multiply_convert_fusion
  675.2 35.3 %all_gather.18 = bf16[64,7168]{1,0:T(8,128)(2,1)} all-gather(bf16[64,896]{1,0:T(8,128)(2,1)S(1)} %get-tuple-element.9), channel_id=1, replica_groups=mesh['seq'=8,'batch'=4] {'seq'}, dimensions={1}, use_global_device_ids=true | all-gather | bytes 1032192 | tf_op jit(solution)/shard_map/all_gather | solution.py:123
  710.6 0.1 broadcast_add_fusion
  710.6 0.1 reshape.346
  710.7 0.1 eq.74
  711.5 27.6 %all-gather.11.cloned.1.call-done = bf16[256,7168]{1,0:T(8,128)(2,1)} async-done(((bf16[64,7168]{1,0:T(8,128)(2,1)}), bf16[256,7168]{1,0:T(8,128)(2,1)}) %all-gather.11.cloned.1.call-update) | async-done | bytes 3670032 | tf_op jit(solution)/shard_map/all_gather | solution.py:129
  739.1 14.0 %fusion.80 = (f32[256]{0:T(256)S(1)}, f32[256,2048]{1,0:T(8,128)S(1)}) fusion(bf16[256,7168]{1,0:T(8,128)(2,1)} %all-gather.11.cloned.1.call-done, bf16[2048,7168]{1,0:T(8,128)(2,1)} %param.27), kind=kOutput, calls=%fused_computation.94 | convolution fusion | flops 7516717056 | bytes 35128320 | tf_op jit(solution)/shard_map/rd,vd->rv/dot_general | solution.py:127
  753.1 39.3 %pmax.15 = f32[256]{0:T(256)S(1)} all-reduce(f32[256]{0:T(256)S(1)} %get-tuple-element.15), channel_id=1, replica_groups=mesh['seq'=8,'batch'=4] {'seq','batch'}, use_global_device_ids=true, to_apply=%region_13.14 | all-reduce | flops 256 | bytes 2048 | tf_op jit(solution)/shard_map/pmax | solution.py:143
  792.4 0.4 exponential_reduce_fusion
  792.8 5.3 gather_fusion
  798.2 1.9 select_reduce_fusion
  800.1 41.0 %all-reduce = (f32[256]{0:T(256)S(1)}, f32[256]{0:T(256)S(1)}) all-reduce(f32[256]{0:T(256)S(1)} %select_reduce_fusion, f32[256]{0:T(256)S(1)} %exponential_reduce_fusion), channel_id=1, replica_groups=mesh['seq'=8,'batch'=4] {'seq','batch'}, use_global_device_ids=true, to_apply=%region_11.12 | all-reduce | flops 512 | bytes 4096 | tf_op jit(solution)/shard_map/psum | solution.py:144
  841.1 1.9 gather_fusion.1
  843.0 0.1 reshape.347
  843.1 1.1 fusion.78
  (43 shorter events, 0.3 us)
Async XLA Ops:
  7.2 2.0 copy-start
  7.2 5.2 copy-start.11
  7.2 54.8 %all-gather.7.cloned.1.call-start = ((), (), s32[]{:S(2)}) async-start(), calls=%async_computation.4 | async-start | bytes 2359296 | tf_op jit(solution)/shard_map/all_gather | solution.py:53
  9.1 178.0 %all-gather.5.cloned.1.call-start = ((), (), s32[]{:S(2)}) async-start(), calls=%async_computation.3 | async-start | bytes 9437184 | tf_op jit(solution)/shard_map/all_gather | solution.py:52
  11.6 53.9 %copy-start.9 = (bf16[1,64,64]{2,1,0:T(8,128)(2,1)S(1)}, bf16[1,64,64]{2,1,0:T(8,128)(2,1)}, u32[]{:S(2)}) copy-start(bf16[1,64,64]{2,1,0:T(8,128)(2,1)} %param.23) | copy-start | bytes 24580
  11.6 403.8 %all-gather.9.cloned.1.call-start = ((), (), s32[]{:S(2)}) async-start(), calls=%async_computation.5 | async-start | bytes 18874368 | tf_op jit(solution)/shard_map/all_gather | solution.py:96
  12.3 467.5 %reduce-scatter.6.cloned.1.call-start = ((), (), s32[]{:S(2)}) async-start(), calls=%async_computation.7 | async-start | bytes 73728 | tf_op jit(solution)/shard_map/reduce_scatter | solution.py:101
  15.2 54.4 %copy-start.7 = (bf16[1,1024,64]{1,2,0:T(8,128)(2,1)S(1)}, bf16[1,1024,64]{1,2,0:T(8,128)(2,1)}, u32[]{:S(2)}) copy-start(bf16[1,1024,64]{1,2,0:T(8,128)(2,1)} %param.21) | copy-start | bytes 393220
  62.0 3.5 copy-start.3
  69.6 117.6 %copy-start.8 = (bf16[1,64,512]{2,1,0:T(8,128)(2,1)S(1)}, bf16[1,64,512]{2,1,0:T(8,128)(2,1)}, u32[]{:S(2)}) copy-start(bf16[1,64,512]{2,1,0:T(8,128)(2,1)} %param.22) | copy-start | bytes 196612
  82.9 115.0 %copy-start.5 = (bf16[1,1024,512]{2,1,0:T(8,128)(2,1)S(1)}, bf16[1,1024,512]{2,1,0:T(8,128)(2,1)}, u32[]{:S(2)}) copy-start(bf16[1,1024,512]{2,1,0:T(8,128)(2,1)} %param.20) | copy-start | bytes 3145732
  287.9 282.8 %reduce-scatter.4.cloned.1.call-start = ((), (), s32[]{:S(2)}) async-start(), calls=%async_computation.6 | async-start | bytes 4718592 | tf_op jit(solution)/shard_map/reduce_scatter | solution.py:100
  442.5 128.2 %copy-start.4 = (bf16[16,512,128]{2,1,0:T(8,128)(2,1)S(1)}, bf16[16,512,128]{2,1,0:T(8,128)(2,1)}, u32[]{:S(2)}) copy-start(bf16[16,512,128]{2,1,0:T(8,128)(2,1)} %param.19) | copy-start | bytes 6291460
  442.5 210.7 %reduce-scatter.8.cloned.1.call-start = ((), (), s32[]{:S(2)}) async-start(), calls=%async_computation.8 | async-start | bytes 2064384 | tf_op jit(solution)/shard_map/reduce_scatter | solution.py:114
  572.9 80.3 %copy-start.6 = (bf16[64,896]{1,0:T(8,128)(2,1)S(1)}, bf16[64,896]{1,0:T(8,128)(2,1)}, u32[]{:S(2)}) copy-start(bf16[64,896]{1,0:T(8,128)(2,1)} %param.24) | copy-start | bytes 344068
  586.4 124.3 %copy-start.10 = (s32[4,64]{1,0:T(4,128)S(1)}, s32[4,64]{1,0:T(4,128)}, u32[]{:S(2)}) copy-start(s32[4,64]{1,0:T(4,128)} %param.29) | copy-start | bytes 3076
  586.4 152.6 %all-gather.11.cloned.1.call-start = ((), (), s32[]{:S(2)}) async-start(), calls=%async_computation.9 | async-start | bytes 4587520 | tf_op jit(solution)/shard_map/all_gather | solution.py:129
  753.1 39.3 %copy-start.2 = (f32[256,2048]{1,0:T(8,128)}, f32[256,2048]{1,0:T(8,128)S(1)}, u32[]{:S(2)}) copy-start(f32[256,2048]{1,0:T(8,128)S(1)} %get-tuple-element.16) | copy-start | bytes 6291460
  792.8 51.4 %copy-start.1 = (bf16[16,128,512]{2,1,0:T(8,128)(2,1)S(1)}, bf16[16,128,512]{2,1,0:T(8,128)(2,1)}, u32[]{:S(2)}) copy-start(bf16[16,128,512]{2,1,0:T(8,128)(2,1)} %param.18) | copy-start | bytes 6291460
Sparse Core Ops, SparseCore 0:
  10.1 51.8 all-gather.6
  64.1 122.9 all-gather.4
  189.3 226.0 all-gather.8
  419.2 60.6 reduce-scatter.5
  483.3 87.3 reduce-scatter.3
  586.6 66.5 reduce-scatter.7
  710.7 28.3 all-gather.10
where the time goes:
time: 852 us; the launch traced here: 851 us
  waiting for transfers between devices  499 us (59%)
  blocking collectives  172 us (20%)
  matrix products  121 us (14%)
  other arithmetic  27.2 us (3%)
  local copies, waits for them, and re-layouts  15.8 us (2%)
  between operations  15.7 us (2%)
    all_gather x1, waiting for transfers between devices, body(): lax.all_gather(absorb_v, 'seq', axis=0, tiled=True)  127 us
    all_gather x1, waiting for transfers between devices, body(): lax.all_gather(query_latent, 'seq', axis=2, tiled=True)  104 us
    reduce_scatter x1, waiting for transfers between devices, body(): lax.psum_scatter(projected, 'seq', scatter_dimension=1, tiled=True)  90 us
    reduce_scatter x1, waiting for transfers between devices, body(): lax.psum_scatter(branch_term, 'seq', scatter_dimension=1, tiled=True)  65.9 us
    all_gather x1, waiting for transfers between devices, body(): lax.all_gather(q_rope, 'seq', axis=2, tiled=True)  46.8 us
    psum x1, blocking collectives, body(): lax.psum((jnp.sum(jnp.exp(logits - best[:, None]), axis=1), picked), ('se...  41 us
    pmax x1, blocking collectives, body(): best = lax.pmax(local_best, ('seq', 'batch'))  39.3 us
    pmax x1, blocking collectives, body(): row_top = lax.pmax(local_top, 'seq')  37.2 us
  transfers between devices with their start and end apart: 7, of which 7 were waited for; matrix products, arithmetic and copies ran while one was open for 14% of the time, Pallas kernels for 0%

commit v1 on v0

--- a/solution.py
+++ b/solution.py
@@ -7,6 +7,21 @@
 masked_value = -1e30
 norm_epsilon = 1e-06
 highest = lax.Precision.HIGHEST
+
+
+def on_each_block(shard, axis, dim, make, out_dim):
+    ways, here, step = (lax.axis_size(axis), lax.axis_index(axis), shard.shape[dim])
+    results = []
+    for far in range(ways):
+        arriving = (
+            lax.ppermute(shard, axis, [(d, (d + 1) % ways) for d in range(ways)])
+            if far + 1 < ways
+            else shard
+        )
+        results.append(make(shard, (here - far) % ways * step))
+        shard = arriving
+    line = jnp.concatenate(results[::-1], axis=out_dim)
+    return jnp.roll(line, (here + 1) * results[0].shape[out_dim], axis=out_dim)
 
 
 def ancestry_of(parents):
@@ -124,11 +139,14 @@
     hidden_out = stream_mine.astype(jnp.bfloat16)
     vocab_rows = lm_head.shape[0]
     vocab_first = lax.axis_index(("seq", "batch")) * vocab_rows
-    logits = jnp.einsum(
-        "rd,vd->rv",
-        lax.all_gather(normed, "batch", axis=0, tiled=True),
-        lm_head,
-        preferred_element_type=jnp.float32,
+    logits = on_each_block(
+        normed,
+        "batch",
+        0,
+        lambda part, offset: jnp.einsum(
+            "rd,vd->rv", part, lm_head, preferred_element_type=jnp.float32
+        ),
+        0,
     )
     request_total = parent.shape[0]
     parent_rows = (

time: 852 us -> 919 us (1.079)
  matrix products: 121 us -> 168 us
    dot_general x1 -> x4, matrix products: 14 us -> 60.3 us  [body(): jnp.einsum('rd,vd->rv', part, lm_head, preferred_element_type=jnp.float32)]
    ppermute x0 -> x3, waiting for transfers between devices: none -> 37.8 us  [on_each_block(): lax.ppermute(shard, axis, [(d, (d + 1) % ways) for d in range(ways)])]
    all_gather x1 -> x0, waiting for transfers between devices: 27.6 us -> none  [body(): lax.all_gather(normed, 'batch', axis=0, tiled=True)]
  transfers between devices with their start and end apart: 7 -> 9, of which waited for: 7 -> 9; matrix products, arithmetic and copies ran while one was open for 14% -> 13% of each run, Pallas kernels for 0% -> 0%
where the time goes in v1:
time: 919 us; the launch traced here: 910 us
  waiting for transfers between devices  507 us (55%)
  blocking collectives  169 us (18%)
  matrix products  168 us (18%)
  other arithmetic  29.9 us (3%)
  local copies, waits for them, and re-layouts  19.2 us (2%)
  between operations  16.2 us (2%)
    all_gather x1, waiting for transfers between devices, body(): lax.all_gather(absorb_v, 'seq', axis=0, tiled=True)  126 us
    all_gather x1, waiting for transfers between devices, body(): lax.all_gather(query_latent, 'seq', axis=2, tiled=True)  104 us
    reduce_scatter x1, waiting for transfers between devices, body(): lax.psum_scatter(projected, 'seq', scatter_dimension=1, tiled=True)  90 us
    reduce_scatter x1, waiting for transfers between devices, body(): lax.psum_scatter(branch_term, 'seq', scatter_dimension=1, tiled=True)  65.9 us
    dot_general x4, matrix products, body(): jnp.einsum('rd,vd->rv', part, lm_head, preferred_element_type=jnp.float32)  60.3 us
    all_gather x1, waiting for transfers between devices, body(): lax.all_gather(q_rope, 'seq', axis=2, tiled=True)  46.8 us
    psum x1, blocking collectives, body(): lax.psum((jnp.sum(jnp.exp(logits - best[:, None]), axis=1), picked), ('se...  42.3 us
    ppermute x3, waiting for transfers between devices, on_each_block(): lax.ppermute(shard, axis, [(d, (d + 1) % ways) for d in range(ways)])  37.8 us
  transfers between devices with their start and end apart: 9, of which 9 were waited for; matrix products, arithmetic and copies ran while one was open for 13% of the time, Pallas kernels for 0%

profile of v1, /device:TPU:0, one launch (start us, length us, event | category | flops | bytes accessed | tf_op | source)
XLA Modules:
  0.0 909.6 jit_solution(1986408705411407247)
XLA Ops:
  7.2 1.9 copy.79
  9.2 2.4 fusion.25
  11.7 0.7 all-gather.8.cloned.1.call-update
  12.4 0.2 fusion.68
  12.7 0.2 convolution_add_fusion.5
  12.9 0.2 fusion.81
  13.0 0.2 convolution_add_fusion.4
  13.2 0.2 fusion.82
  13.4 0.2 convolution_add_fusion.3
  13.5 0.2 fusion.83
  13.7 0.2 convolution_add_fusion.2
  13.9 0.2 fusion.84
  14.0 0.2 convolution_add_fusion.1
  14.2 0.2 fusion.41
  14.4 0.1 copy.82
  15.2 46.8 %all-gather.6.cloned.1.call-done = bf16[1,64,128,64]{3,1,0,2:T(8,128)(2,1)} async-done(((bf16[1,64,16,64]{3,1,0,2:T(8,128)(2,1)}), bf16[1,64,128,64]{3,1,0,2:T(8,128)(2,1)}) %all-gather.6.cloned.1.call-update) | async-done | bytes 1048592 | tf_op jit(solution)/shard_map/all_gather | solution.py:68
  62.0 3.5 copy.80
  65.5 4.1 fusion.20
  69.6 13.3 %fusion.42 = f32[1024,64,128]{0,2,1:T(8,128)} fusion(bf16[1,64,128,64]{2,3,1,0:T(8,128)(2,1)S(1)} %copy.80, bf16[1,1024,64]{1,2,0:T(8,128)(2,1)S(1)} %copy-done.7), kind=kOutput, calls=%fused_computation.42 | convolution fusion | flops 1073741824 | bytes 34734080 | tf_op jit(solution)/shard_map/rihe,rte->rhit/dot_general | solution.py:73
  82.9 104.3 %all-gather.4.cloned.1.call-done = bf16[1,64,128,512]{3,1,0,2:T(8,128)(2,1)} async-done(((bf16[1,64,16,512]{3,1,0,2:T(8,128)(2,1)}), bf16[1,64,128,512]{3,1,0,2:T(8,128)(2,1)}) %all-gather.4.cloned.1.call-update) | async-done | bytes 8388624 | tf_op jit(solution)/shard_map/all_gather | solution.py:67
  187.1 10.7 %fusion.80 = (f32[128,64]{1,0:T(8,128)S(1)}, f32[1,128,64,64]{2,3,1,0:T(8,128)}) fusion(f32[64,64,128]{1,0,2:T(8,128)} %fusion.20, bf16[1,64,512]{2,1,0:T(8,128)(2,1)S(1)} %copy-done.8, bf16[1,64,128,512]{3,1,0,2:T(8,128)(2,1)} %all-gather.4.cloned.1.call-done, pred[64,64]{0,1:T(8,128)(4,1)S(1)} %copy.82), kind=kOutput, calls=%fused_computation.103 | convolution fusion | flops 538959872 | bytes 12685312 | tf_op jit(solution)/shard_map/rihc,rjc->rhij/dot_general | solution.py:79
  197.9 32.5 %bitcast_reduce_fusion = (f32[128,64]{0,1:T(8,128)S(1)}, f32[1,1024,64,128]{1,3,2,0:T(8,128)}) fusion(f32[1024,64,128]{0,2,1:T(8,128)} %fusion.42, bf16[1,1024,512]{2,1,0:T(8,128)(2,1)S(1)} %copy-done.5, bf16[1,64,128,512]{3,1,0,2:T(8,128)(2,1)} %all-gather.4.cloned.1.call-done, pred[1024]{0:T(1024)(128)(4,1)S(1)} %add_compare_fusion), kind=kOutput, calls=%fused_computation.3 | convolution fusion | flops 8623480832 | bytes 76579840 | tf_op jit(solution)/shard_map/rihc,rtc->rhit/dot_general | solution.py:70
  230.4 37.5 %pmax.14 = f32[1,128,64]{1,2,0:T(8,128)S(1)} all-reduce(f32[1,128,64]{1,2,0:T(8,128)S(1)} %maximum_bitcast_fusion), channel_id=1, replica_groups=mesh['seq'=8,'batch'=4] {'seq'}, use_global_device_ids=true, to_apply=%region_2.3 | all-reduce | flops 8192 | bytes 65536 | tf_op jit(solution)/shard_map/pmax | solution.py:89
  268.0 20.5 %fusion.2 = (f32[128,64]{0,1:T(8,128)S(1)}, bf16[128,64,1024]{2,0,1:T(8,128)(2,1)}) fusion(f32[1,1024,64,128]{1,3,2,0:T(8,128)} %get-tuple-element.14, f32[128,64]{0,1:T(8,128)S(1)} %bitcast.166), kind=kLoop, calls=%fused_computation.8 | loop fusion | flops 25157632 | bytes 50397184 | tf_op jit(solution)/shard_map/reduce_sum | solution.py:91
  288.5 0.7 copy.89
  289.3 126.0 %all-gather.8.cloned.1.call-done = bf16[128,512,128]{2,1,0:T(8,128)(2,1)} async-done(((bf16[16,512,128]{2,1,0:T(8,128)(2,1)}), bf16[128,512,128]{2,1,0:T(8,128)(2,1)}) %all-gather.8.cloned.1.call-update) | async-done | bytes 16777232 | tf_op jit(solution)/shard_map/all_gather | solution.py:111
  415.3 27.1 %fusion.17 = f32[1,128,64,128]{3,2,1,0:T(8,128)} fusion(bf16[128,512,128]{2,1,0:T(8,128)(2,1)} %all-gather.8.cloned.1.call-done, bf16[128,64,1024]{2,0,1:T(8,128)(2,1)} %get-tuple-element.10, bf16[1,1024,512]{2,1,0:T(8,128)(2,1)S(1)} %copy-done.5), kind=kOutput, calls=%fused_computation.21 | convolution fusion | flops 9663676416 | bytes 38797312 | tf_op jit(solution)/shard_map/rhic,hcn->rhin/dot_general | solution.py:108
  442.5 0.1 constant_dynamic-slice_fusion.2
  442.6 1.3 fusion.47
  443.9 0.1 copy.100
  444.0 35.8 %reduce-scatter.6.cloned.1.call-done = f32[1,16,64]{2,0,1:T(1,128)} async-done(((f32[1,128,64]{2,0,1:T(1,128)}), f32[1,16,64]{2,0,1:T(1,128)}) %reduce-scatter.6.cloned.1.call-update) | async-done | bytes 4112 | tf_op jit(solution)/shard_map/reduce_scatter | solution.py:116
  479.7 0.8 copy.91
  480.6 90.0 %reduce-scatter.4.cloned.1.call-done = f32[1,16,64,128]{3,2,1,0:T(8,128)} async-done(((f32[1,128,64,128]{3,2,1,0:T(8,128)}), f32[1,16,64,128]{3,2,1,0:T(8,128)}) %reduce-scatter.4.cloned.1.call-update) | async-done | bytes 524304 | tf_op jit(solution)/shard_map/reduce_scatter | solution.py:115
  570.6 2.0 fusion.38
  572.6 0.2 copy.93
  572.8 13.5 %fusion.52 = f32[64,7168]{1,0:T(8,128)} fusion(bf16[2048,7168]{1,0:T(8,128)(2,1)} %param.25, bf16[8,8,16,128]{3,2,1,0:T(8,128)(2,1)S(1)} %bitcast.165), kind=kOutput, calls=%fused_computation.50 | convolution fusion | flops 1879048192 | bytes 31457280 | tf_op jit(solution)/shard_map/dot_general | solution.py:126
  586.3 0.8 dynamic_slice.22
  587.1 65.9 %reduce-scatter.8.cloned.1.call-done = f32[64,896]{1,0:T(8,128)} async-done(((f32[64,7168]{1,0:T(8,128)}), f32[64,896]{1,0:T(8,128)}) %reduce-scatter.8.cloned.1.call-update) | async-done | bytes 229392 | tf_op jit(solution)/shard_map/reduce_scatter | solution.py:129
  653.1 1.1 multiply_reduce_fusion
  654.1 19.4 %psum.21 = f32[64]{0:T(128)S(1)} all-reduce(f32[64]{0:T(128)S(1)} %multiply_reduce_fusion), channel_id=1, replica_groups=mesh['seq'=8,'batch'=4] {'seq'}, use_global_device_ids=true, to_apply=%region_9.10 | all-reduce | flops 64 | bytes 512 | tf_op jit(solution)/shard_map/psum | solution.py:132
  673.5 1.6 multiply_convert_fusion
  675.1 32.8 %all_gather.15 = bf16[64,7168]{1,0:T(8,128)(2,1)S(1)} all-gather(bf16[64,896]{1,0:T(8,128)(2,1)S(1)} %get-tuple-element.11), channel_id=1, replica_groups=mesh['seq'=8,'batch'=4] {'seq'}, dimensions={1}, use_global_device_ids=true | all-gather | bytes 1032192 | tf_op jit(solution)/shard_map/all_gather | solution.py:138
  707.9 12.8 %collective-permute-done = bf16[64,7168]{1,0:T(8,128)(2,1)S(1)} collective-permute-done((bf16[64,7168]{1,0:T(8,128)(2,1)S(1)}, bf16[64,7168]{1,0:T(8,128)(2,1)S(1)}, u32[]{:S(2)}, u32[]{:S(2)}) %collective-permute-start) | collective-permute-done | bytes 917536 | tf_op jit(solution)/shard_map/ppermute | solution.py:17
  720.7 12.9 %collective-permute-done.1 = bf16[64,7168]{1,0:T(8,128)(2,1)} collective-permute-done((bf16[64,7168]{1,0:T(8,128)(2,1)S(1)}, bf16[64,7168]{1,0:T(8,128)(2,1)}, u32[]{:S(2)}, u32[]{:S(2)}) %collective-permute-start.1) | collective-permute-done | bytes 917536 | tf_op jit(solution)/shard_map/ppermute | solution.py:17
  733.7 0.1 reshape.346
  733.8 0.1 eq.77
  734.6 12.1 %collective-permute-done.2 = bf16[64,7168]{1,0:T(8,128)(2,1)S(1)} collective-permute-done((bf16[64,7168]{1,0:T(8,128)(2,1)}, bf16[64,7168]{1,0:T(8,128)(2,1)S(1)}, u32[]{:S(2)}, u32[]{:S(2)}) %collective-permute-start.2) | collective-permute-done | bytes 917536 | tf_op jit(solution)/shard_map/ppermute | solution.py:17
  746.7 15.0 %constant_dynamic-update-slice_fusion.7 = (f32[512,2048]{1,0:T(8,128)}, f32[64,2048]{1,0:T(8,128)S(1)}) fusion(bf16[64,7168]{1,0:T(8,128)(2,1)S(1)} %collective-permute-done.2, bf16[2048,7168]{1,0:T(8,128)(2,1)} %param.27), kind=kOutput, calls=%fused_computation.79 | convolution fusion | flops 1879048192 | bytes 31326208 | tf_op jit(solution)/shard_map/rd,vd->rv/dot_general | solution.py:146
  761.7 15.2 %constant_dynamic-update-slice_fusion.6 = (f32[512,2048]{1,0:T(8,128)}, f32[64,2048]{1,0:T(8,128)S(1)}) fusion(f32[512,2048]{1,0:T(8,128)} %get-tuple-element.17, bf16[64,7168]{1,0:T(8,128)(2,1)} %collective-permute-done.1, bf16[2048,7168]{1,0:T(8,128)(2,1)} %param.27), kind=kOutput, calls=%fused_computation.78 | convolution fusion | flops 1879048192 | bytes 31326208 | tf_op jit(solution)/shard_map/rd,vd->rv/dot_general | solution.py:146
  776.9 15.0 %constant_dynamic-update-slice_fusion.5 = (f32[512,2048]{1,0:T(8,128)}, f32[64,2048]{1,0:T(8,128)S(1)}) fusion(f32[512,2048]{1,0:T(8,128)} %get-tuple-element.19, bf16[64,7168]{1,0:T(8,128)(2,1)S(1)} %collective-permute-done, bf16[2048,7168]{1,0:T(8,128)(2,1)} %param.27), kind=kOutput, calls=%fused_computation.77 | convolution fusion | flops 1879048192 | bytes 31326208 | tf_op jit(solution)/shard_map/rd,vd->rv/dot_general | solution.py:146
  791.9 15.0 %constant_dynamic-update-slice_fusion.4 = (f32[512,2048]{1,0:T(8,128)}, f32[64,2048]{1,0:T(8,128)S(1)}) fusion(f32[512,2048]{1,0:T(8,128)} %get-tuple-element.21, bf16[64,7168]{1,0:T(8,128)(2,1)S(1)} %all_gather.15, bf16[2048,7168]{1,0:T(8,128)(2,1)} %param.27), kind=kOutput, calls=%fused_computation.76 | convolution fusion | flops 1879048192 | bytes 31326208 | tf_op jit(solution)/shard_map/rd,vd->rv/dot_general | solution.py:146
  806.9 0.8 constant_dynamic-update-slice_fusion.3
  807.8 0.8 constant_dynamic-update-slice_fusion.2
  808.6 0.8 constant_dynamic-update-slice_fusion.1
  809.4 0.8 constant_dynamic-update-slice_fusion
  810.3 1.8 fusion.79
  812.1 37.1 %pmax.15 = f32[256]{0:T(256)S(1)} all-reduce(f32[256]{0:T(256)S(1)} %get-tuple-element.7), channel_id=1, replica_groups=mesh['seq'=8,'batch'=4] {'seq','batch'}, use_global_device_ids=true, to_apply=%region_13.14 | all-reduce | flops 256 | bytes 2048 | tf_op jit(solution)/shard_map/pmax | solution.py:161
  849.2 0.4 exponential_reduce_fusion
  849.7 5.3 gather_fusion
  855.0 1.9 select_reduce_fusion
  856.9 42.3 %all-reduce = (f32[256]{0:T(256)S(1)}, f32[256]{0:T(256)S(1)}) all-reduce(f32[256]{0:T(256)S(1)} %select_reduce_fusion, f32[256]{0:T(256)S(1)} %exponential_reduce_fusion), channel_id=1, replica_groups=mesh['seq'=8,'batch'=4] {'seq','batch'}, use_global_device_ids=true, to_apply=%region_11.12 | all-reduce | flops 512 | bytes 4096 | tf_op jit(solution)/shard_map/psum | solution.py:162
  899.2 1.9 gather_fusion.1
  901.2 0.1 reshape.347
  901.2 1.1 fusion.78
  (54 shorter events, 0.7 us)
Async XLA Ops:
  7.2 2.0 copy-start
  7.2 5.2 copy-start.11
  7.2 54.8 %all-gather.6.cloned.1.call-start = ((), (), s32[]{:S(2)}) async-start(), calls=%async_computation.4 | async-start | bytes 2359296 | tf_op jit(solution)/shard_map/all_gather | solution.py:68
  9.1 178.0 %all-gather.4.cloned.1.call-start = ((), (), s32[]{:S(2)}) async-start(), calls=%async_computation.3 | async-start | bytes 9437184 | tf_op jit(solution)/shard_map/all_gather | solution.py:67
  11.6 53.9 %copy-start.9 = (bf16[1,64,64]{2,1,0:T(8,128)(2,1)S(1)}, bf16[1,64,64]{2,1,0:T(8,128)(2,1)}, u32[]{:S(2)}) copy-start(bf16[1,64,64]{2,1,0:T(8,128)(2,1)} %param.23) | copy-start | bytes 24580
  11.6 403.7 %all-gather.8.cloned.1.call-start = ((), (), s32[]{:S(2)}) async-start(), calls=%async_computation.5 | async-start | bytes 18874368 | tf_op jit(solution)/shard_map/all_gather | solution.py:111
  12.3 467.4 %reduce-scatter.6.cloned.1.call-start = ((), (), s32[]{:S(2)}) async-start(), calls=%async_computation.7 | async-start | bytes 73728 | tf_op jit(solution)/shard_map/reduce_scatter | solution.py:116
  15.2 54.4 %copy-start.7 = (bf16[1,1024,64]{1,2,0:T(8,128)(2,1)S(1)}, bf16[1,1024,64]{1,2,0:T(8,128)(2,1)}, u32[]{:S(2)}) copy-start(bf16[1,1024,64]{1,2,0:T(8,128)(2,1)} %param.21) | copy-start | bytes 393220
  62.0 3.5 copy-start.3
  69.6 117.6 %copy-start.8 = (bf16[1,64,512]{2,1,0:T(8,128)(2,1)S(1)}, bf16[1,64,512]{2,1,0:T(8,128)(2,1)}, u32[]{:S(2)}) copy-start(bf16[1,64,512]{2,1,0:T(8,128)(2,1)} %param.22) | copy-start | bytes 196612
  82.9 115.0 %copy-start.5 = (bf16[1,1024,512]{2,1,0:T(8,128)(2,1)S(1)}, bf16[1,1024,512]{2,1,0:T(8,128)(2,1)}, u32[]{:S(2)}) copy-start(bf16[1,1024,512]{2,1,0:T(8,128)(2,1)} %param.20) | copy-start | bytes 3145732
  289.2 281.4 %reduce-scatter.4.cloned.1.call-start = ((), (), s32[]{:S(2)}) async-start(), calls=%async_computation.6 | async-start | bytes 4718592 | tf_op jit(solution)/shard_map/reduce_scatter | solution.py:115
  442.4 128.2 %copy-start.4 = (bf16[16,512,128]{2,1,0:T(8,128)(2,1)S(1)}, bf16[16,512,128]{2,1,0:T(8,128)(2,1)}, u32[]{:S(2)}) copy-start(bf16[16,512,128]{2,1,0:T(8,128)(2,1)} %param.19) | copy-start | bytes 6291460
  442.4 210.6 %reduce-scatter.8.cloned.1.call-start = ((), (), s32[]{:S(2)}) async-start(), calls=%async_computation.8 | async-start | bytes 2064384 | tf_op jit(solution)/shard_map/reduce_scatter | solution.py:129
  572.8 80.3 %copy-start.6 = (bf16[64,896]{1,0:T(8,128)(2,1)S(1)}, bf16[64,896]{1,0:T(8,128)(2,1)}, u32[]{:S(2)}) copy-start(bf16[64,896]{1,0:T(8,128)(2,1)} %param.24) | copy-start | bytes 344068
  572.8 161.0 %copy-start.10 = (s32[4,64]{1,0:T(4,128)S(1)}, s32[4,64]{1,0:T(4,128)}, u32[]{:S(2)}) copy-start(s32[4,64]{1,0:T(4,128)} %param.29) | copy-start | bytes 3076
  707.9 12.8 %collective-permute-start = (bf16[64,7168]{1,0:T(8,128)(2,1)S(1)}, bf16[64,7168]{1,0:T(8,128)(2,1)S(1)}, u32[]{:S(2)}, u32[]{:S(2)}) collective-permute-start(bf16[64,7168]{1,0:T(8,128)(2,1)S(1)} %all_gather.15), channel_id=1, source_target_pairs={{0,1},{1,2},{2,3},{3,0},{4,5},{5,6},{6,7},{7,4},{8,9},{9,10},{10,1... | collective-permute-start | bytes 2752520 | tf_op jit(solution)/shard_map/ppermute | solution.py:17
  720.7 12.9 %collective-permute-start.1 = (bf16[64,7168]{1,0:T(8,128)(2,1)S(1)}, bf16[64,7168]{1,0:T(8,128)(2,1)}, u32[]{:S(2)}, u32[]{:S(2)}) collective-permute-start(bf16[64,7168]{1,0:T(8,128)(2,1)S(1)} %collective-permute-done), channel_id=1, source_target_pairs={{0,1},{1,2},{2,3},{3,0},{4,5},{5,6},{6,7},{7,4},{8,9},{9,10},{10,1... | collective-permute-start | bytes 2752520 | tf_op jit(solution)/shard_map/ppermute | solution.py:17
  733.6 13.0 %collective-permute-start.2 = (bf16[64,7168]{1,0:T(8,128)(2,1)}, bf16[64,7168]{1,0:T(8,128)(2,1)S(1)}, u32[]{:S(2)}, u32[]{:S(2)}) collective-permute-start(bf16[64,7168]{1,0:T(8,128)(2,1)} %collective-permute-done.1), channel_id=1, source_target_pairs={{0,1},{1,2},{2,3},{3,0},{4,5},{5,6},{6,7},{7,4},{8,9},{9,10},{10,1... | collective-permute-start | bytes 2752520 | tf_op jit(solution)/shard_map/ppermute | solution.py:17
  812.1 37.1 %copy-start.2 = (f32[256,2048]{1,0:T(8,128)}, f32[256,2048]{1,0:T(8,128)S(1)}, u32[]{:S(2)}) copy-start(f32[256,2048]{1,0:T(8,128)S(1)} %get-tuple-element.8) | copy-start | bytes 6291460
  849.6 52.7 %copy-start.1 = (bf16[16,128,512]{2,1,0:T(8,128)(2,1)S(1)}, bf16[16,128,512]{2,1,0:T(8,128)(2,1)}, u32[]{:S(2)}) copy-start(bf16[16,128,512]{2,1,0:T(8,128)(2,1)} %param.18) | copy-start | bytes 6291460
Sparse Core Ops, SparseCore 0:
  10.1 51.8 all-gather.5
  64.1 122.9 all-gather.3
  189.3 225.9 all-gather.7
  419.1 60.5 reduce-scatter.5
  483.2 87.3 reduce-scatter.3
  586.4 66.5 reduce-scatter.7
